TPU v7x, 32 devices: a whole 2x2x4 slice. The times are simulated.
32 devices in a mesh: dp: 4 (over z), vocab: 8 (over y, x, core).
Axes of the slice: x: 2, y: 2, z: 4, core: 2. Of those that a mesh axis runs over, the one named last changes fastest.
Arguments:
- hidden: bfloat16 [2560, 4096], P(('dp', 'vocab')), may hold values from -192 to 192, as said below
- out_weight: bfloat16 [4096, 20480], P('dp', 'vocab'), may hold values from -0.09375 to 0.09375
- labels: int32 [2560], P('dp'), may hold values from 0 to 20479
- text_mask: int32 [2560], P('dp'), may hold values from 0 to 1, as said below
Outputs:
- token_loss: float32 [2560], P('dp')
- mean_loss: float32 [], replicated
Inputs may be any that keep to these rules, and one draw needn't show every extreme that they name: The hidden states are of moderate size in most rows, possibly larger in a few. `text_mask`: vision and text tokens come in runs of 16 aligned tokens.
All inputs are finite; a program needn't handle non-finite values.
Results may differ from a plain program's by a relative error of at most 0.0003.
Values may be sent and summed in bfloat16 or wider, within the bound.
No kernel may reach another device: no remote copies, remote signals or barrier semaphores. Data moves between devices by JAX's collectives and lax.ppermute only.
A program may use at most 128 MiB of HBM per device.

v0:
```python
import jax
import jax.numpy as jnp
from jax import lax
from jax.sharding import PartitionSpec as P


def combined_all(part, axis, combine):
    gathered = jax.tree.map(lambda a: lax.all_gather(a, axis), part)

    def take(source):
        return jax.tree.map(lambda a: lax.dynamic_index_in_dim(a, source, 0, False), gathered)

    return lax.fori_loop(
        1, lax.axis_size(axis), lambda source, state: combine(state, take(source)), take(0)
    )


def shards(hidden, out_weight, labels, text_mask):
    gathered = lax.all_gather(hidden, "vocab", axis=0, tiled=True)
    width_here = out_weight.shape[1]
    first_column = lax.axis_index("vocab") * width_here
    weight_full = lax.all_gather(out_weight, "dp", axis=0, tiled=True)
    logits = jnp.dot(gathered, weight_full, preferred_element_type=jnp.float32)
    columns = jnp.arange(width_here, dtype=jnp.int32)
    local_targets = labels - first_column
    picked = jnp.sum(
        jnp.where(columns[None, :] == local_targets[:, None], logits, jnp.float32(0.0)), axis=1
    )
    local_top = jnp.max(logits, axis=1)
    weights_text = text_mask.astype(jnp.float32)
    tally = lax.psum(jnp.sum(weights_text), "dp")
    local_total = jnp.sum(jnp.exp(logits - local_top[:, None]), axis=1)

    def combine(first, second):
        upper = jnp.maximum(first[0], second[0])
        summed = first[1] * jnp.exp(first[0] - upper) + second[1] * jnp.exp(second[0] - upper)
        return (upper, summed, first[2] + second[2])

    row_top, exp_total, label_logit = combined_all(
        (local_top, local_total, picked), "vocab", combine
    )
    token_loss = weights_text * (row_top + jnp.log(exp_total) - label_logit)
    loss_sum = lax.psum(jnp.sum(token_loss), "dp")
    mean_loss = loss_sum / jnp.maximum(tally, jnp.float32(1.0))
    return (token_loss, mean_loss)


def solution(mesh):
    in_specs = (P(("dp", "vocab"), None), P("dp", "vocab"), P("dp"), P("dp"))
    out_specs = (P("dp"), P())
    return jax.shard_map(shards, mesh=mesh, in_specs=in_specs, out_specs=out_specs, check_vma=False)
```

profile of v0, /device:TPU:0, one launch (start us, length us, event | category | flops | bytes accessed | tf_op | source)
XLA Modules:
  0.0 480.1 jit_solution(2350190988107568957)
XLA Ops:
  7.2 0.0 all-gather.9.cloned.1.call-start
  7.2 0.7 all-gather.9.cloned.1.call-update
  7.9 0.0 all-gather.11.cloned.1.call-start
  7.9 0.7 all-gather.11.cloned.1.call-update
  8.7 0.7 broadcast_subtract_fusion
  9.3 44.3 %all-gather.9.cloned.1.call-done = bf16[640,4096]{1,0:T(8,128)(2,1)} async-done(((bf16[80,4096]{1,0:T(8,128)(2,1)}), bf16[640,4096]{1,0:T(8,128)(2,1)}) %all-gather.9.cloned.1.call-update) | async-done | bytes 5242896 | tf_op jit(solution)/shard_map/all_gather | solution.py:19
  53.6 358.4 %all-gather.11.cloned.1.call-done = bf16[4096,2560]{1,0:T(8,128)(2,1)} async-done(((bf16[1024,2560]{1,0:T(8,128)(2,1)}), bf16[4096,2560]{1,0:T(8,128)(2,1)}) %all-gather.11.cloned.1.call-update) | async-done | bytes 20971536 | tf_op jit(solution)/shard_map/all_gather | solution.py:22
  412.0 18.6 %fusion.1 = (f32[640]{0:T(1024)S(1)}, f32[640,2560]{1,0:T(8,128)S(1)}) fusion(bf16[640,4096]{1,0:T(8,128)(2,1)} %all-gather.9.cloned.1.call-done, bf16[4096,2560]{1,0:T(8,128)(2,1)} %all-gather.11.cloned.1.call-done), kind=kOutput, calls=%fused_computation.17 | convolution fusion | flops 13423410176 | bytes 32770560 | tf_op jit(solution)/shard_map/dot_general | solution.py:23
  430.6 0.0 copy-start
  430.6 2.2 select_reduce_fusion
  432.8 9.0 %all-gather.5 = f32[8,1,640]{2,1,0:T(1,128)S(1)} all-gather(f32[1,1,640]{2,1,0:T(1,128)S(1)} %reshape.19), channel_id=4, replica_groups=mesh['dp'=4,'vocab'=8] {'vocab'}, dimensions={0}, use_global_device_ids=true | all-gather | bytes 23040 | tf_op jit(solution)/shard_map/all_gather | solution.py:8
  441.9 9.0 %all-gather.4 = f32[8,1,640]{2,1,0:T(1,128)S(1)} all-gather(f32[1,1,640]{2,1,0:T(1,128)S(1)} %reshape.17), channel_id=3, replica_groups=mesh['dp'=4,'vocab'=8] {'vocab'}, dimensions={0}, use_global_device_ids=true | all-gather | bytes 23040 | tf_op jit(solution)/shard_map/all_gather | solution.py:8
  450.9 8.1 %all-gather.3 = f32[8,1,640]{2,1,0:T(1,128)S(1)} all-gather(f32[1,1,640]{2,1,0:T(1,128)S(1)} %reshape.15), channel_id=2, replica_groups=mesh['dp'=4,'vocab'=8] {'vocab'}, dimensions={0}, use_global_device_ids=true | all-gather | bytes 23040 | tf_op jit(solution)/shard_map/all_gather | solution.py:8
  459.0 0.8 while.19
  459.8 0.0 copy-done
  459.8 1.3 fusion
  461.1 9.8 %all-reduce = (f32[]{:T(128)}, f32[]{:T(128)}) all-reduce(f32[]{:T(128)} %get-tuple-element.203, f32[]{:T(128)} %get-tuple-element.207), channel_id=1, replica_groups=mesh['dp'=4,'vocab'=8] {'dp'}, use_global_device_ids=true, to_apply=%region_6.7 | all-reduce | flops 2 | bytes 16 | tf_op jit(solution)/shard_map/psum | solution.py:43
  (37 shorter events, 0.5 us)
Async XLA Ops:
  7.2 46.4 %all-gather.9.cloned.1.call-start = ((), (), s32[]{:S(2)}) async-start(), calls=%async_computation | async-start | bytes 5898240 | tf_op jit(solution)/shard_map/all_gather | solution.py:19
  7.9 404.1 %all-gather.11.cloned.1.call-start = ((), (), s32[]{:S(2)}) async-start(), calls=%async_computation.1 | async-start | bytes 26214400 | tf_op jit(solution)/shard_map/all_gather | solution.py:22
  430.6 29.2 %copy-start = (s32[640]{0:T(1024)S(1)}, s32[640]{0:T(1024)}, u32[]{:S(2)}) copy-start(s32[640]{0:T(1024)} %param.9) | copy-start | bytes 7684
Sparse Core Ops, SparseCore 0:
  9.9 43.6 all-gather.8
  55.2 356.8 all-gather.10
where the time goes:
time: 480 us
  waiting for transfers between devices  404 us (84%)
  blocking collectives  36 us (8%)
  matrix products  18.6 us (4%)
  between operations  16.5 us (3%)
    all_gather x1, waiting for transfers between devices, shards(): weight_full = lax.all_gather(out_weight, 'dp', axis=0, tiled=True)  358 us
    all_gather x1, waiting for transfers between devices, shards(): gathered = lax.all_gather(hidden, 'vocab', axis=0, tiled=True)  44.3 us
    all_gather x3, blocking collectives, combined_all(): gathered = jax.tree.map(lambda a: lax.all_gather(a, axis), part)  26.2 us
    dot_general x1, matrix products, shards(): logits = jnp.dot(gathered, weight_full, preferred_element_type=jnp.float32)  18.6 us
    psum x1, blocking collectives, shards(): loss_sum = lax.psum(jnp.sum(token_loss), 'dp')  9.84 us
  transfers between devices with their start and end apart: 2, of which 2 were waited for; matrix products, arithmetic and copies ran while one was open for 0% of the time, Pallas kernels for 0%

commit v1 on v0

--- a/solution.py
+++ b/solution.py
@@ -16,7 +16,14 @@
 
 
 def shards(hidden, out_weight, labels, text_mask):
-    gathered = lax.all_gather(hidden, "vocab", axis=0, tiled=True)
+    ring = [hidden]
+    for hop in range(7):
+        ring.append(lax.ppermute(ring[-1], "vocab", [(dev, (dev + 1) % 8) for dev in range(8)]))
+    gathered = jnp.roll(
+        jnp.concatenate(ring[::-1], axis=0),
+        (lax.axis_index("vocab") + 1) * ring[0].shape[0],
+        axis=0,
+    )
     width_here = out_weight.shape[1]
     first_column = lax.axis_index("vocab") * width_here
     weight_full = lax.all_gather(out_weight, "dp", axis=0, tiled=True)

time: 480 us -> 438 us (0.912)
  waiting for transfers between devices: 404 us -> 340 us
  local copies, waits for them, and re-layouts: 0.4 us -> 21.1 us
    all_gather x1, waiting for transfers between devices: 358 us -> 263 us  [shards(): weight_full = lax.all_gather(out_weight, 'dp', axis=0, tiled=True)]
    ppermute x0 -> x7, waiting for transfers between devices: none -> 76.5 us  [shards(): lax.ppermute(ring[-1], 'vocab', [(dev, (dev + 1) % 8) for dev in range(8)])]
    all_gather x1 -> x0, waiting for transfers between devices: 44.3 us -> none  [shards(): gathered = lax.all_gather(hidden, 'vocab', axis=0, tiled=True)]
    unnamed x8 -> x29, local copies, waits for them, and re-layouts: 0.03 us -> 19.8 us
  transfers between devices with their start and end apart: 2 -> 8, of which waited for: 2 -> 8; matrix products, arithmetic and copies ran while one was open for 0% -> 5% of each run, Pallas kernels for 0% -> 0%
where the time goes in v1:
time: 438 us; the launch traced here: 437 us
  waiting for transfers between devices  340 us (78%)
  blocking collectives  36 us (8%)
  local copies, waits for them, and re-layouts  21.1 us (5%)
  matrix products  18.6 us (4%)
  between operations  16.5 us (4%)
    all_gather x1, waiting for transfers between devices, shards(): weight_full = lax.all_gather(out_weight, 'dp', axis=0, tiled=True)  263 us
    ppermute x7, waiting for transfers between devices, shards(): lax.ppermute(ring[-1], 'vocab', [(dev, (dev + 1) % 8) for dev in range(8)])  76.5 us
    all_gather x3, blocking collectives, combined_all(): gathered = jax.tree.map(lambda a: lax.all_gather(a, axis), part)  26.2 us
    unnamed x29, local copies, waits for them, and re-layouts  19.8 us
    dot_general x1, matrix products, shards(): logits = jnp.dot(gathered, weight_full, preferred_element_type=jnp.float32)  18.6 us
    psum x1, blocking collectives, shards(): loss_sum = lax.psum(jnp.sum(token_loss), 'dp')  9.85 us
  transfers between devices with their start and end apart: 8, of which 8 were waited for; matrix products, arithmetic and copies ran while one was open for 5% of the time, Pallas kernels for 0%

profile of v1, /device:TPU:0, one launch (start us, length us, event | category | flops | bytes accessed | tf_op | source)
XLA Modules:
  0.0 437.3 jit_solution(4332656094396267264)
XLA Ops:
  7.2 0.0 copy-start
  7.2 0.0 all-gather.8.cloned.1.call-start
  7.2 0.7 all-gather.8.cloned.1.call-update
  7.9 0.5 collective-permute-start
  8.5 11.3 %collective-permute-done = bf16[80,4096]{1,0:T(8,128)(2,1)S(1)} collective-permute-done((bf16[80,4096]{1,0:T(8,128)(2,1)}, bf16[80,4096]{1,0:T(8,128)(2,1)S(1)}, u32[]{:S(2)}, u32[]{:S(2)}) %collective-permute-start) | collective-permute-done | bytes 655392 | tf_op jit(solution)/shard_map/ppermute | solution.py:21
  19.8 0.0 collective-permute-start.1
  19.8 10.9 %collective-permute-done.1 = bf16[80,4096]{1,0:T(8,128)(2,1)S(1)} collective-permute-done((bf16[80,4096]{1,0:T(8,128)(2,1)S(1)}, bf16[80,4096]{1,0:T(8,128)(2,1)S(1)}, u32[]{:S(2)}, u32[]{:S(2)}) %collective-permute-start.1) | collective-permute-done | bytes 655392 | tf_op jit(solution)/shard_map/ppermute | solution.py:21
  30.7 0.0 collective-permute-start.2
  30.7 10.9 %collective-permute-done.2 = bf16[80,4096]{1,0:T(8,128)(2,1)S(1)} collective-permute-done((bf16[80,4096]{1,0:T(8,128)(2,1)S(1)}, bf16[80,4096]{1,0:T(8,128)(2,1)S(1)}, u32[]{:S(2)}, u32[]{:S(2)}) %collective-permute-start.2) | collective-permute-done | bytes 655392 | tf_op jit(solution)/shard_map/ppermute | solution.py:21
  41.6 0.0 collective-permute-start.3
  41.6 10.9 %collective-permute-done.3 = bf16[80,4096]{1,0:T(8,128)(2,1)S(1)} collective-permute-done((bf16[80,4096]{1,0:T(8,128)(2,1)S(1)}, bf16[80,4096]{1,0:T(8,128)(2,1)S(1)}, u32[]{:S(2)}, u32[]{:S(2)}) %collective-permute-start.3) | collective-permute-done | bytes 655392 | tf_op jit(solution)/shard_map/ppermute | solution.py:21
  52.5 0.0 collective-permute-start.4
  52.5 10.9 %collective-permute-done.4 = bf16[80,4096]{1,0:T(8,128)(2,1)S(1)} collective-permute-done((bf16[80,4096]{1,0:T(8,128)(2,1)S(1)}, bf16[80,4096]{1,0:T(8,128)(2,1)S(1)}, u32[]{:S(2)}, u32[]{:S(2)}) %collective-permute-start.4) | collective-permute-done | bytes 655392 | tf_op jit(solution)/shard_map/ppermute | solution.py:21
  63.4 0.0 copy-start.1
  63.4 0.8 copy-done.1
  64.3 0.0 collective-permute-start.5
  64.3 11.0 %collective-permute-done.5 = bf16[80,4096]{1,0:T(8,128)(2,1)} collective-permute-done((bf16[80,4096]{1,0:T(8,128)(2,1)S(1)}, bf16[80,4096]{1,0:T(8,128)(2,1)}, u32[]{:S(2)}, u32[]{:S(2)}) %collective-permute-start.5) | collective-permute-done | bytes 655392 | tf_op jit(solution)/shard_map/ppermute | solution.py:21
  75.3 0.0 collective-permute-start.6
  75.3 0.0 copy-start.2
  75.3 0.8 broadcast_subtract_fusion
  76.1 10.5 %collective-permute-done.6 = bf16[80,4096]{1,0:T(8,128)(2,1)} collective-permute-done((bf16[80,4096]{1,0:T(8,128)(2,1)}, bf16[80,4096]{1,0:T(8,128)(2,1)}, u32[]{:S(2)}, u32[]{:S(2)}) %collective-permute-start.6) | collective-permute-done | bytes 655392 | tf_op jit(solution)/shard_map/ppermute | solution.py:21
  86.5 2.0 constant_dynamic-update-slice_fusion.15
  88.5 2.0 constant_dynamic-update-slice_fusion.14
  90.5 2.0 constant_dynamic-update-slice_fusion.13
  92.5 0.9 constant_dynamic-update-slice_fusion.12
  93.4 0.9 constant_dynamic-update-slice_fusion.11
  94.3 0.9 constant_dynamic-update-slice_fusion.10
  95.2 0.9 constant_dynamic-update-slice_fusion.9
  96.1 0.0 copy-done
  96.1 1.0 constant_dynamic-update-slice_fusion.8
  97.1 2.0 constant_dynamic-update-slice_fusion.7
  99.0 2.0 constant_dynamic-update-slice_fusion.6
  101.0 0.0 copy-done.2
  101.0 0.9 constant_dynamic-update-slice_fusion.5
  101.9 0.9 constant_dynamic-update-slice_fusion.4
  102.8 0.9 constant_dynamic-update-slice_fusion.3
  103.7 0.9 constant_dynamic-update-slice_fusion.2
  104.6 0.9 constant_dynamic-update-slice_fusion.1
  105.5 0.9 constant_dynamic-update-slice_fusion
  106.4 0.0 copy-start.3
  106.4 262.8 %all-gather.8.cloned.1.call-done = bf16[4096,2560]{1,0:T(8,128)(2,1)} async-done(((bf16[1024,2560]{1,0:T(8,128)(2,1)}), bf16[4096,2560]{1,0:T(8,128)(2,1)}) %all-gather.8.cloned.1.call-update) | async-done | bytes 20971536 | tf_op jit(solution)/shard_map/all_gather | solution.py:29
  369.1 18.6 %fusion.4 = (f32[640]{0:T(1024)S(1)}, f32[640,2560]{1,0:T(8,128)S(1)}) fusion(bf16[4096,2560]{1,0:T(8,128)(2,1)} %all-gather.8.cloned.1.call-done, bf16[1280,4096]{1,0:T(8,128)(2,1)} %constant_dynamic-update-slice_fusion, s32[]{:T(128)S(6)} %select_n.34), kind=kOutput, calls=%fused_computation.36 | convolution fusion | flops 13423410176 | bytes 32770564 | tf_op jit(solution)/shard_map/dot_general | solution.py:30
  387.8 2.2 select_reduce_fusion
  389.9 9.0 %all-gather.5 = f32[8,1,640]{2,1,0:T(1,128)S(1)} all-gather(f32[1,1,640]{2,1,0:T(1,128)S(1)} %reshape.19), channel_id=4, replica_groups=mesh['dp'=4,'vocab'=8] {'vocab'}, dimensions={0}, use_global_device_ids=true | all-gather | bytes 23040 | tf_op jit(solution)/shard_map/all_gather | solution.py:8
  399.0 9.0 %all-gather.4 = f32[8,1,640]{2,1,0:T(1,128)S(1)} all-gather(f32[1,1,640]{2,1,0:T(1,128)S(1)} %reshape.17), channel_id=3, replica_groups=mesh['dp'=4,'vocab'=8] {'vocab'}, dimensions={0}, use_global_device_ids=true | all-gather | bytes 23040 | tf_op jit(solution)/shard_map/all_gather | solution.py:8
  408.0 8.2 %all-gather.3 = f32[8,1,640]{2,1,0:T(1,128)S(1)} all-gather(f32[1,1,640]{2,1,0:T(1,128)S(1)} %reshape.15), channel_id=2, replica_groups=mesh['dp'=4,'vocab'=8] {'vocab'}, dimensions={0}, use_global_device_ids=true | all-gather | bytes 23040 | tf_op jit(solution)/shard_map/all_gather | solution.py:8
  416.2 0.8 while.19
  417.0 0.0 copy-done.3
  417.0 1.3 fusion.3
  418.3 9.9 %all-reduce = (f32[]{:T(128)}, f32[]{:T(128)}) all-reduce(f32[]{:T(128)} %get-tuple-element.203, f32[]{:T(128)} %get-tuple-element.207), channel_id=1, replica_groups=mesh['dp'=4,'vocab'=8] {'dp'}, use_global_device_ids=true, to_apply=%region_6.7 | all-reduce | flops 2 | bytes 16 | tf_op jit(solution)/shard_map/psum | solution.py:50
  (37 shorter events, 0.5 us)
Async XLA Ops:
  7.2 89.0 %copy-start = (bf16[80,4096]{1,0:T(8,128)(2,1)S(1)}, bf16[80,4096]{1,0:T(8,128)(2,1)}, u32[]{:S(2)}) copy-start(bf16[80,4096]{1,0:T(8,128)(2,1)} %param.6) | copy-start | bytes 1966084
  7.2 362.0 %all-gather.8.cloned.1.call-start = ((), (), s32[]{:S(2)}) async-start(), calls=%async_computation | async-start | bytes 26214400 | tf_op jit(solution)/shard_map/all_gather | solution.py:29
  7.9 11.9 %collective-permute-start = (bf16[80,4096]{1,0:T(8,128)(2,1)}, bf16[80,4096]{1,0:T(8,128)(2,1)S(1)}, u32[]{:S(2)}, u32[]{:S(2)}) collective-permute-start(bf16[80,4096]{1,0:T(8,128)(2,1)} %param.6), channel_id=1, source_target_pairs={{0,1},{1,2},{2,3},{3,4},{4,5},{5,6},{6,7},{7,0},{8,9},{9,10},{10,1... | collective-permute-start | bytes 1966088 | tf_op jit(solution)/shard_map/ppermute | solution.py:21
  19.8 10.9 %collective-permute-start.1 = (bf16[80,4096]{1,0:T(8,128)(2,1)S(1)}, bf16[80,4096]{1,0:T(8,128)(2,1)S(1)}, u32[]{:S(2)}, u32[]{:S(2)}) collective-permute-start(bf16[80,4096]{1,0:T(8,128)(2,1)S(1)} %collective-permute-done), channel_id=1, source_target_pairs={{0,1},{1,2},{2,3},{3,4},{4,5},{5,6},{6,7},{7,0},{8,9},{9,10},{10,1... | collective-permute-start | bytes 1966088 | tf_op jit(solution)/shard_map/ppermute | solution.py:21
  30.7 10.9 %collective-permute-start.2 = (bf16[80,4096]{1,0:T(8,128)(2,1)S(1)}, bf16[80,4096]{1,0:T(8,128)(2,1)S(1)}, u32[]{:S(2)}, u32[]{:S(2)}) collective-permute-start(bf16[80,4096]{1,0:T(8,128)(2,1)S(1)} %collective-permute-done.1), channel_id=1, source_target_pairs={{0,1},{1,2},{2,3},{3,4},{4,5},{5,6},{6,7},{7,0},{8,9},{9,10},{10,1... | collective-permute-start | bytes 1966088 | tf_op jit(solution)/shard_map/ppermute | solution.py:21
  41.6 10.9 %collective-permute-start.3 = (bf16[80,4096]{1,0:T(8,128)(2,1)S(1)}, bf16[80,4096]{1,0:T(8,128)(2,1)S(1)}, u32[]{:S(2)}, u32[]{:S(2)}) collective-permute-start(bf16[80,4096]{1,0:T(8,128)(2,1)S(1)} %collective-permute-done.2), channel_id=1, source_target_pairs={{0,1},{1,2},{2,3},{3,4},{4,5},{5,6},{6,7},{7,0},{8,9},{9,10},{10,1... | collective-permute-start | bytes 1966088 | tf_op jit(solution)/shard_map/ppermute | solution.py:21
  52.5 10.9 %collective-permute-start.4 = (bf16[80,4096]{1,0:T(8,128)(2,1)S(1)}, bf16[80,4096]{1,0:T(8,128)(2,1)S(1)}, u32[]{:S(2)}, u32[]{:S(2)}) collective-permute-start(bf16[80,4096]{1,0:T(8,128)(2,1)S(1)} %collective-permute-done.3), channel_id=1, source_target_pairs={{0,1},{1,2},{2,3},{3,4},{4,5},{5,6},{6,7},{7,0},{8,9},{9,10},{10,1... | collective-permute-start | bytes 1966088 | tf_op jit(solution)/shard_map/ppermute | solution.py:21
  63.4 0.9 copy-start.1
  64.3 11.0 %collective-permute-start.5 = (bf16[80,4096]{1,0:T(8,128)(2,1)S(1)}, bf16[80,4096]{1,0:T(8,128)(2,1)}, u32[]{:S(2)}, u32[]{:S(2)}) collective-permute-start(bf16[80,4096]{1,0:T(8,128)(2,1)S(1)} %collective-permute-done.4), channel_id=1, source_target_pairs={{0,1},{1,2},{2,3},{3,4},{4,5},{5,6},{6,7},{7,0},{8,9},{9,10},{10,1... | collective-permute-start | bytes 1966088 | tf_op jit(solution)/shard_map/ppermute | solution.py:21
  75.3 11.2 %collective-permute-start.6 = (bf16[80,4096]{1,0:T(8,128)(2,1)}, bf16[80,4096]{1,0:T(8,128)(2,1)}, u32[]{:S(2)}, u32[]{:S(2)}) collective-permute-start(bf16[80,4096]{1,0:T(8,128)(2,1)} %collective-permute-done.5), channel_id=1, source_target_pairs={{0,1},{1,2},{2,3},{3,4},{4,5},{5,6},{6,7},{7,0},{8,9},{9,10},{10,1... | collective-permute-start | bytes 1966088 | tf_op jit(solution)/shard_map/ppermute | solution.py:21
  75.3 25.7 %copy-start.2 = (bf16[80,4096]{1,0:T(8,128)(2,1)S(1)}, bf16[80,4096]{1,0:T(8,128)(2,1)}, u32[]{:S(2)}) copy-start(bf16[80,4096]{1,0:T(8,128)(2,1)} %copy-done.1) | copy-start | bytes 1966084
  106.4 310.6 %copy-start.3 = (s32[640]{0:T(1024)S(1)}, s32[640]{0:T(1024)}, u32[]{:S(2)}) copy-start(s32[640]{0:T(1024)} %param.9) | copy-start | bytes 7684
Sparse Core Ops, SparseCore 0:
  9.6 359.5 all-gather.7
